TPU v7x, 256 devices: a whole 4x4x8 slice. The times are simulated.
256 devices in a mesh: dp: 256 (over z, x, y, core).
Axes of the slice: x: 4, y: 4, z: 8, core: 2. Of those that a mesh axis runs over, the one named last changes fastest.
Arguments:
- images: bfloat16 [1024, 92, 4096], P('dp'), may hold values from -6 to 6
- layer_gain: float32 [4096], replicated, may hold values from 0.5 to 1.5
- in_weight: bfloat16 [4096, 1024], replicated, may hold values from -1 to 1
- out_weight: bfloat16 [1024, 1024], replicated, may hold values from -1 to 1
- text_embed: bfloat16 [1024, 1024], P('dp'), may hold values from -6 to 6
- pair_index: int32 [1024], P('dp'), may hold values from 0 to 1023, each once
- logit_scale: float32 [1], replicated, may hold values from 30 to 200
Outputs:
- loss: float32 [1], replicated
- grad_norm: float32 [1], replicated
- update_image: float32 [1024, 1024], P('dp')
- update_text: float32 [1024, 1024], P('dp')
Inputs may be any that keep to these rules, and one draw needn't show every extreme that they name: Image i is paired with text row pair_index[i]; every text row is paired with exactly one image.
All inputs are finite; a program needn't handle non-finite values.
Results may differ from a plain program's by a relative error of at most 0.0086.
Values may be sent and summed in bfloat16 or wider, within the bound.
A program may use at most 64 MiB of HBM per device.

v0:
```python
import jax
import jax.numpy as jnp
from jax import lax
from jax.sharding import Mesh
from jax.sharding import PartitionSpec as P

DP = ("dp_0", "dp_1", "dp_2", "dp_3")
EPS_UNIT = 1e-06
EPS_LAYER = 1e-05


def from_everyone(array, axis):
    size = lax.axis_size(axis)
    return lax.all_to_all(
        jnp.broadcast_to(array[None], (size, *array.shape)), axis, 0, 0, tiled=True
    )


def laid_out(blocks, dim):
    lengths = list(blocks.shape[1:])
    lengths[dim] *= blocks.shape[0]
    return jnp.moveaxis(blocks, 0, dim).reshape(lengths)


def whole_of(array, axes, dim):
    far, near = axes
    first = from_everyone(array, far)
    blocks = jnp.swapaxes(from_everyone(first, near), 0, 1)
    return laid_out(blocks.reshape(-1, *array.shape), dim)


def turned_gather(arrays, axis, dims):
    turned = [jnp.moveaxis(a, dim, 0) for a, dim in zip(arrays, dims)]
    both = jnp.concatenate([t.reshape(len(t), -1) for t in turned], axis=1)
    filled, at, finished = (lax.all_gather(both, axis, axis=0, tiled=True), 0, [])
    for t, dim in zip(turned, dims):
        section = filled[:, at : at + t[0].size].reshape(-1, *t.shape[1:])
        finished.append(jnp.moveaxis(section, 0, dim))
        at += t[0].size
    return tuple(finished)


def over_copies(array, axis):
    return from_everyone(array, axis).sum(axis=0)


def one_axis_at_a_time(array, axes):
    far, near = axes
    return over_copies(over_copies(array, near), far)


def in_one(arrays, axis):
    ends = [0]
    for a in arrays:
        ends.append(ends[-1] + a.size)
    subtotal = one_axis_at_a_time(jnp.concatenate([a.ravel() for a in arrays]), axis)
    return tuple((subtotal[b:e].reshape(a.shape) for a, b, e in zip(arrays, ends, ends[1:])))


def unit_rows(matrix):
    length = jnp.sqrt(jnp.sum(matrix * matrix, axis=1, keepdims=True) + EPS_UNIT)
    return (matrix / length, length)


def unit_backward(grad_unit, unit_vec, length):
    return (grad_unit - unit_vec * jnp.sum(unit_vec * grad_unit, axis=1, keepdims=True)) / length


def per_device(images, layer_gain, in_weight, out_weight, text_embed, pair_index, logit_scale):
    multiplier = logit_scale[0]
    local_rows = images.shape[0]
    devices = lax.axis_size(DP)
    total_rows = local_rows * devices
    width = out_weight.shape[1]
    first_row = lax.axis_index(DP) * local_rows
    text_unit, text_len = unit_rows(text_embed.astype(jnp.float32))
    text_vec = text_unit.astype(jnp.bfloat16)
    all_text = whole_of(text_vec, (("dp_0", "dp_1"), ("dp_2", "dp_3")), 0)
    values = images.astype(jnp.float32)
    average = jnp.mean(values, axis=-1, keepdims=True)
    centered = values - average
    variance = jnp.mean(centered * centered, axis=-1, keepdims=True)
    normed = (centered * lax.rsqrt(variance + EPS_LAYER) * layer_gain).astype(jnp.bfloat16)
    flattened = normed.reshape(-1, normed.shape[-1])
    hidden = jax.nn.gelu(
        jnp.dot(flattened, in_weight, preferred_element_type=jnp.float32), approximate=True
    )
    pooled = jnp.mean(hidden.reshape(local_rows, images.shape[1], -1), axis=1).astype(jnp.bfloat16)
    image_emb = jnp.dot(pooled, out_weight, preferred_element_type=jnp.float32)
    image_unit, image_len = unit_rows(image_emb)
    image_vec = image_unit.astype(jnp.bfloat16)
    scores = multiplier * lax.dot_general(
        image_vec, all_text, (((1,), (1,)), ((), ())), preferred_element_type=jnp.float32
    )
    row_high = jnp.max(scores, axis=1, keepdims=True)
    row_lse = row_high[:, 0] + jnp.log(jnp.sum(jnp.exp(scores - row_high), axis=1))
    column_ids = jnp.arange(total_rows, dtype=jnp.int32)
    target = column_ids[None, :] == pair_index[:, None]
    positive = jnp.sum(jnp.where(target, scores, jnp.zeros_like(scores)), axis=1)
    all_images = whole_of(image_vec, (("dp_0", "dp_1"), ("dp_2", "dp_3")), 0)
    all_row_lse, all_pairs = turned_gather((row_lse, pair_index.astype(jnp.float32)), DP, (0, 0))
    text_scores = multiplier * lax.dot_general(
        text_vec, all_images, (((1,), (1,)), ((), ())), preferred_element_type=jnp.float32
    )
    text_high = jnp.max(text_scores, axis=1, keepdims=True)
    col_lse_own = text_high[:, 0] + jnp.log(jnp.sum(jnp.exp(text_scores - text_high), axis=1))
    own_ids = (first_row + jnp.arange(local_rows, dtype=jnp.int32)).astype(jnp.float32)
    text_target = all_pairs[None, :] == own_ids[:, None]
    text_weights = (
        jnp.exp(text_scores - all_row_lse[None, :])
        + jnp.exp(text_scores - col_lse_own[:, None])
        - 2.0 * text_target.astype(jnp.float32)
    ).astype(jnp.bfloat16)
    grad_text_unit = multiplier * jnp.dot(
        text_weights, all_images, preferred_element_type=jnp.float32
    )
    col_lse_all = whole_of(col_lse_own, (("dp_0", "dp_1"), ("dp_2", "dp_3")), 0)
    weights = (
        jnp.exp(scores - row_lse[:, None])
        + jnp.exp(scores - col_lse_all[None, :])
        - 2.0 * target.astype(jnp.float32)
    ).astype(jnp.bfloat16)
    loss_part = jnp.sum(row_lse) + jnp.sum(col_lse_own) - 2.0 * jnp.sum(positive)
    grad_image_unit = multiplier * jnp.dot(weights, all_text, preferred_element_type=jnp.float32)
    grad_image = unit_backward(grad_image_unit, image_unit, image_len)
    grad_text = unit_backward(grad_text_unit, text_unit, text_len)
    square_part = jnp.sum(grad_image * grad_image) + jnp.sum(grad_text * grad_text)
    loss_total, squares = in_one((loss_part, square_part), (("dp_0", "dp_1"), ("dp_2", "dp_3")))
    loss = loss_total / (2.0 * total_rows)
    factor = lax.rsqrt(squares / (2.0 * total_rows * width) + 1e-06)
    return (loss.reshape(1), jnp.sqrt(squares).reshape(1), grad_image * factor, grad_text * factor)


def solution(mesh):
    torus = Mesh(mesh.devices.reshape(8, 4, 4, 2), ("dp_0", "dp_1", "dp_2", "dp_3"))
    return jax.shard_map(
        per_device,
        mesh=torus,
        in_specs=(P(DP, None, None), P(), P(), P(), P(DP, None), P(DP), P()),
        out_specs=(P(), P(), P(DP, None), P(DP, None)),
        check_vma=False,
    )
```

profile of v0, /device:TPU:1, one launch (start us, length us, event | category | flops | bytes accessed | tf_op | source)
XLA Modules:
  0.0 258.0 jit_solution(7069101414245393673)
XLA Ops:
  3.2 11.9 %all-to-all-start = ((bf16[32,4,1024]{2,1,0:T(4,128)(2,1)}), bf16[32,4,1024]{2,1,0:T(4,128)(2,1)S(1)}, u32[]{:S(2)}, u32[]{:S(2)}) async-start(bf16[32,4,1024]{2,1,0:T(4,128)(2,1)} %broadcast_in_dim.20), calls=%async_computation | async-start | bytes 524288 | tf_op jit(solution)/shard_map/all_to_all | solution.py:14
  15.0 3.3 %convert_reduce_fusion = f32[4,92]{0,1:T(8,128)S(1)} fusion(bf16[4,92,4096]{2,0,1:T(4,128)(2,1)} %param.7), kind=kLoop, calls=%fused_computation.1 | loop fusion | flops 3014288 | bytes 3016128 | tf_op jit(solution)/shard_map/reduce_sum | solution.py:80
  18.3 2.1 fusion.2
  20.4 3.2 %fusion.4 = bf16[4,92,4096]{2,0,1:T(4,128)(2,1)S(1)} fusion(bf16[4,92,4096]{2,0,1:T(4,128)(2,1)S(1)} %copy-done.1, f32[4096]{0:T(1024)S(1)} %copy-done.4, f32[4,92]{0,1:T(8,128)S(1)} %add_rsqrt_fusion, f32[4,92]{0,1:T(8,128)S(1)} %broadcast_multiply_fusion), kind=kLoop, calls=%fused_computation.6 | loop fusion | flops 7536640 | bytes 6048640 | tf_op jit(solution)/shard_map/convert_element_type | solution.py:83
  23.7 3.3 %copy.27 = bf16[4,92,4096]{2,1,0:T(8,128)(2,1)} copy(bf16[4,92,4096]{2,0,1:T(4,128)(2,1)S(1)} %fusion.4) | data formatting | bytes 6029312 | tf_op jit(solution)/shard_map/convert_element_type | solution.py:83
  27.0 3.4 %reshape.128 = bf16[368,4096]{1,0:T(8,128)(2,1)} reshape(bf16[4,92,4096]{2,1,0:T(8,128)(2,1)} %copy.27) | data formatting | bytes 6029312 | tf_op jit(solution)/shard_map/reshape | solution.py:84
  30.4 9.0 %fusion.11 = f32[368,1024]{1,0:T(8,128)} fusion(bf16[368,4096]{1,0:T(8,128)(2,1)} %reshape.128, bf16[4096,1024]{1,0:T(8,128)(2,1)} %param.9), kind=kOutput, calls=%fused_computation.14 | convolution fusion | flops 3090022400 | bytes 12910592 | tf_op jit(solution)/shard_map/dot_general | solution.py:86
  39.3 2.7 %reshape.129 = f32[4,92,1024]{2,1,0:T(8,128)} reshape(f32[368,1024]{1,0:T(8,128)} %fusion.11) | data formatting | bytes 3014656 | tf_op jit(solution)/shard_map/reshape | solution.py:88
  44.3 19.8 %all_to_all.43 = bf16[32,4,1024]{2,1,0:T(4,128)(2,1)S(1)} all-to-all(bf16[32,4,1024]{2,1,0:T(4,128)(2,1)S(1)} %broadcast_in_dim.22), channel_id=1, replica_groups=mesh['dp_0'=8,'dp_1'=4,'dp_2'=4,'dp_3'=2] {'dp_0','dp_1'}, dimensions={0} | all-to-all | bytes 524288 | tf_op jit(solution)/shard_map/all_to_all | solution.py:14
  64.8 33.8 %all_to_all.44 = bf16[8,32,4,1024]{3,2,1,0:T(4,128)(2,1)} all-to-all(bf16[8,32,4,1024]{3,2,1,0:T(4,128)(2,1)S(1)} %broadcast_in_dim.21), channel_id=1, replica_groups=mesh['dp_0'=8,'dp_1'=4,'dp_2'=4,'dp_3'=2] {'dp_2','dp_3'}, dimensions={0} | all-to-all | bytes 4194304 | tf_op jit(solution)/shard_map/all_to_all | solution.py:14
  100.6 5.4 %all-to-all-start.3 = ((bf16[8,32,4,1024]{3,2,1,0:T(4,128)(2,1)}), bf16[8,32,4,1024]{3,2,1,0:T(4,128)(2,1)}, u32[]{:S(2)}, u32[]{:S(2)}) async-start(bf16[8,32,4,1024]{3,2,1,0:T(4,128)(2,1)} %broadcast_in_dim.23), calls=%async_computation.3 | async-start | bytes 4194304 | tf_op jit(solution)/shard_map/all_to_all | solution.py:14
  106.7 4.1 %copy.28 = bf16[32,8,4,1024]{3,2,1,0:T(4,128)(2,1)} copy(bf16[32,8,4,1024]{3,2,0,1:T(4,128)(2,1)} %bitcast.35) | data formatting | bytes 4194304 | tf_op jit(solution)/shard_map/transpose | solution.py:28
  110.8 4.0 %reshape_reshape.6 = bf16[1024,1024]{1,0:T(8,128)(2,1)} reshape(bf16[32,8,4,1024]{3,2,1,0:T(4,128)(2,1)} %copy.28) | data formatting | bytes 4194304 | tf_op jit(solution)/shard_map/reshape;reshape | solution.py:22
  114.8 17.6 %all-to-all-done.3 = bf16[8,32,4,1024]{3,2,1,0:T(4,128)(2,1)} async-done(((bf16[8,32,4,1024]{3,2,1,0:T(4,128)(2,1)}), bf16[8,32,4,1024]{3,2,1,0:T(4,128)(2,1)}, u32[]{:S(2)}, u32[]{:S(2)}) %all-to-all-start.3) | async-done | bytes 2097184 | tf_op jit(solution)/shard_map/all_to_all | solution.py:14
  132.4 4.1 %copy.29 = bf16[32,8,4,1024]{3,2,1,0:T(4,128)(2,1)} copy(bf16[32,8,4,1024]{3,2,0,1:T(4,128)(2,1)} %bitcast.2) | data formatting | bytes 4194304 | tf_op jit(solution)/shard_map/transpose | solution.py:28
  136.4 4.0 %reshape_reshape.7 = bf16[1024,1024]{1,0:T(8,128)(2,1)} reshape(bf16[32,8,4,1024]{3,2,1,0:T(4,128)(2,1)} %copy.29) | data formatting | bytes 4194304 | tf_op jit(solution)/shard_map/reshape;reshape | solution.py:22
  140.4 2.5 fusion.38
  145.9 3.8 %all-to-all-start.4 = ((f32[32,1,4]{2,1,0:T(1,128)}), f32[32,1,4]{2,1,0:T(1,128)S(1)}, u32[]{:S(2)}, u32[]{:S(2)}) async-start(f32[32,1,4]{2,1,0:T(1,128)} %broadcast_in_dim.25), calls=%async_computation.4 | async-start | bytes 32768 | tf_op jit(solution)/shard_map/all_to_all | solution.py:14
  149.7 63.0 %all-gather = f32[256,4,2]{1,2,0:T(2,128)S(1)} all-gather(f32[1,4,2]{1,2,0:T(2,128)S(1)} %maximum_bitcast_fusion), channel_id=1, replica_groups=mesh['dp_0'=8,'dp_1'=4,'dp_2'=4,'dp_3'=2] {'dp_0','dp_1','dp_2','dp_3'}, dimensions={0}, use_global_device_ids=true | all-gather | bytes 8224 | tf_op jit(solution)/shard_map/all_gather | solution.py:35
  212.9 2.1 multiply_reduce_fusion.1
  215.9 3.4 %all-to-all-start.5 = ((f32[8,1,128]{2,1,0:T(1,128)}), f32[8,1,128]{2,1,0:T(1,128)S(1)}, u32[]{:S(2)}, u32[]{:S(2)}) async-start(f32[8,1,128]{2,1,0:T(1,128)} %reshape.135), calls=%async_computation.5 | async-start | bytes 8192 | tf_op jit(solution)/shard_map/all_to_all | solution.py:14
  225.3 2.1 multiply_reduce_fusion.3
  229.5 7.6 %all_to_all.45 = f32[8,1,2]{2,1,0:T(1,128)S(1)} all-to-all(f32[8,1,2]{2,1,0:T(1,128)S(1)} %broadcast_in_dim.28), channel_id=1, replica_groups=mesh['dp_0'=8,'dp_1'=4,'dp_2'=4,'dp_3'=2] {'dp_2','dp_3'}, dimensions={0} | all-to-all | bytes 128 | tf_op jit(solution)/shard_map/all_to_all | solution.py:14
  237.2 14.6 %all_to_all.46 = f32[32,1,2]{2,1,0:T(1,128)S(1)} all-to-all(f32[32,1,2]{2,1,0:T(1,128)S(1)} %broadcast_in_dim.29), channel_id=1, replica_groups=mesh['dp_0'=8,'dp_1'=4,'dp_2'=4,'dp_3'=2] {'dp_0','dp_1'}, dimensions={0} | all-to-all | bytes 512 | tf_op jit(solution)/shard_map/all_to_all | solution.py:14
  (58 shorter events, 18.3 us)
Async XLA Ops:
  0.6 42.9 %copy-start = (bf16[1024,1024]{1,0:T(8,128)(2,1)S(1)}, bf16[1024,1024]{1,0:T(8,128)(2,1)}, u32[]{:S(2)}) copy-start(bf16[1024,1024]{1,0:T(8,128)(2,1)} %param.10) | copy-start | bytes 6291460
  3.2 41.0 %all-to-all-start = ((bf16[32,4,1024]{2,1,0:T(4,128)(2,1)}), bf16[32,4,1024]{2,1,0:T(4,128)(2,1)S(1)}, u32[]{:S(2)}, u32[]{:S(2)}) async-start(bf16[32,4,1024]{2,1,0:T(4,128)(2,1)} %broadcast_in_dim.20), calls=%async_computation | async-start | bytes 524288 | tf_op jit(solution)/shard_map/all_to_all | solution.py:14
  15.0 3.3 %copy-start.1 = (bf16[4,92,4096]{2,0,1:T(4,128)(2,1)S(1)}, bf16[4,92,4096]{2,0,1:T(4,128)(2,1)}, u32[]{:S(2)}) copy-start(bf16[4,92,4096]{2,0,1:T(4,128)(2,1)} %param.7) | copy-start | bytes 9043972
  18.3 2.1 copy-start.4
  100.6 6.1 %copy-start.5 = (s32[4]{0:T(128)S(1)}, s32[4]{0:T(128)}, u32[]{:S(2)}) copy-start(s32[4]{0:T(128)} %param.12) | copy-start | bytes 52
  100.6 31.8 %all-to-all-start.3 = ((bf16[8,32,4,1024]{3,2,1,0:T(4,128)(2,1)}), bf16[8,32,4,1024]{3,2,1,0:T(4,128)(2,1)}, u32[]{:S(2)}, u32[]{:S(2)}) async-start(bf16[8,32,4,1024]{3,2,1,0:T(4,128)(2,1)} %broadcast_in_dim.23), calls=%async_computation.3 | async-start | bytes 4194304 | tf_op jit(solution)/shard_map/all_to_all | solution.py:14
  140.4 2.5 copy-start.2
  142.9 70.0 %copy-start.3 = (bf16[4,1024]{1,0:T(4,128)(2,1)S(1)}, bf16[4,1024]{1,0:T(4,128)(2,1)}, u32[]{:S(2)}) copy-start(bf16[4,1024]{1,0:T(4,128)(2,1)} %param.11) | copy-start | bytes 24580
  145.9 69.2 %all-to-all-start.4 = ((f32[32,1,4]{2,1,0:T(1,128)}), f32[32,1,4]{2,1,0:T(1,128)S(1)}, u32[]{:S(2)}, u32[]{:S(2)}) async-start(f32[32,1,4]{2,1,0:T(1,128)} %broadcast_in_dim.25), calls=%async_computation.4 | async-start | bytes 32768 | tf_op jit(solution)/shard_map/all_to_all | solution.py:14
  215.9 7.9 %all-to-all-start.5 = ((f32[8,1,128]{2,1,0:T(1,128)}), f32[8,1,128]{2,1,0:T(1,128)S(1)}, u32[]{:S(2)}, u32[]{:S(2)}) async-start(f32[8,1,128]{2,1,0:T(1,128)} %reshape.135), calls=%async_computation.5 | async-start | bytes 8192 | tf_op jit(solution)/shard_map/all_to_all | solution.py:14
where the time goes:
time: 259 us; the launch traced here: 258 us
  blocking collectives  139 us (54%)
  local copies, waits for them, and re-layouts  32.1 us (12%)
  starting transfers between devices  24.5 us (9%)
  waiting for transfers between devices  19.6 us (8%)
  other arithmetic  17 us (7%)
  matrix products  17 us (7%)
  between operations  9.03 us (3%)
    all_to_all x4, blocking collectives, from_everyone(): lax.all_to_all(jnp.broadcast_to(array[None], (size, *array.shape)), axis,...  75.8 us
    all_gather x1, blocking collectives, turned_gather(): lax.all_gather(both, axis, axis=0, tiled=True)  63 us
    all_to_all x4, starting transfers between devices, from_everyone(): lax.all_to_all(jnp.broadcast_to(array[None], (size, *array.shape)), axis,...  24.5 us
    all_to_all x4, waiting for transfers between devices, from_everyone(): lax.all_to_all(jnp.broadcast_to(array[None], (size, *array.shape)), axis,...  19.6 us
    dot_general x1, matrix products, per_device(): jnp.dot(flattened, in_weight, preferred_element_type=jnp.float32)  8.96 us
    transpose x4, local copies, waits for them, and re-layouts, whole_of(): blocks = jnp.swapaxes(from_everyone(first, near), 0, 1)  8.27 us
    another operation x2, local copies, waits for them, and re-layouts, laid_out(): return jnp.moveaxis(blocks, 0, dim).reshape(lengths)  7.93 us
  transfers between devices with their start and end apart: 4, of which 2 were waited for; matrix products, arithmetic and copies ran while one was open for 16% of the time, Pallas kernels for 0%

commit v1 on v0

--- a/solution.py
+++ b/solution.py
@@ -32,7 +32,16 @@
 def turned_gather(arrays, axis, dims):
     turned = [jnp.moveaxis(a, dim, 0) for a, dim in zip(arrays, dims)]
     both = jnp.concatenate([t.reshape(len(t), -1) for t in turned], axis=1)
-    filled, at, finished = (lax.all_gather(both, axis, axis=0, tiled=True), 0, [])
+    filled, at, finished = (
+        jnp.concatenate(
+            lax.all_to_all(
+                jnp.stack([both for _ in range(lax.axis_size(axis))], axis=0), axis, 0, 0
+            ),
+            axis=0,
+        ),
+        0,
+        [],
+    )
     for t, dim in zip(turned, dims):
         section = filled[:, at : at + t[0].size].reshape(-1, *t.shape[1:])
         finished.append(jnp.moveaxis(section, 0, dim))

time: 259 us -> 222 us (0.86)
  blocking collectives: 139 us -> 73.3 us
  waiting for transfers between devices: 19.6 us -> 39.9 us
  starting transfers between devices: 24.5 us -> 32.3 us
    all_gather x1 -> x0, blocking collectives: 63 us -> none  [turned_gather(): lax.all_gather(both, axis, axis=0, tiled=True)]
    all_to_all x0 -> x1, waiting for transfers between devices: none -> 11.1 us  [turned_gather(): lax.all_to_all(jnp.stack([both for _ in range(lax.axis_size(axis))], axis...]
    all_to_all x4, waiting for transfers between devices: 19.6 us -> 28.8 us  [from_everyone(): lax.all_to_all(jnp.broadcast_to(array[None], (size, *array.shape)), axis,...]
    all_to_all x0 -> x1, starting transfers between devices: none -> 5.7 us  [turned_gather(): lax.all_to_all(jnp.stack([both for _ in range(lax.axis_size(axis))], axis...]
  transfers between devices with their start and end apart: 4 -> 5, of which waited for: 2 -> 4; matrix products, arithmetic and copies ran while one was open for 16% -> 19% of each run, Pallas kernels for 0% -> 0%
where the time goes in v1:
time: 222 us; the launch traced here: 221 us
  blocking collectives  73.3 us (33%)
  waiting for transfers between devices  39.9 us (18%)
  local copies, waits for them, and re-layouts  32.9 us (15%)
  starting transfers between devices  32.3 us (15%)
  other arithmetic  17 us (8%)
  matrix products  17 us (8%)
  between operations  9.05 us (4%)
    all_to_all x4, blocking collectives, from_everyone(): lax.all_to_all(jnp.broadcast_to(array[None], (size, *array.shape)), axis,...  73.3 us
    all_to_all x4, waiting for transfers between devices, from_everyone(): lax.all_to_all(jnp.broadcast_to(array[None], (size, *array.shape)), axis,...  28.8 us
    all_to_all x4, starting transfers between devices, from_everyone(): lax.all_to_all(jnp.broadcast_to(array[None], (size, *array.shape)), axis,...  26.6 us
    all_to_all x1, waiting for transfers between devices, turned_gather(): lax.all_to_all(jnp.stack([both for _ in range(lax.axis_size(axis))], axis...  11.1 us
    dot_general x1, matrix products, per_device(): jnp.dot(flattened, in_weight, preferred_element_type=jnp.float32)  8.96 us
    transpose x4, local copies, waits for them, and re-layouts, whole_of(): blocks = jnp.swapaxes(from_everyone(first, near), 0, 1)  8.27 us
    another operation x2, local copies, waits for them, and re-layouts, laid_out(): return jnp.moveaxis(blocks, 0, dim).reshape(lengths)  7.93 us
    all_to_all x1, starting transfers between devices, turned_gather(): lax.all_to_all(jnp.stack([both for _ in range(lax.axis_size(axis))], axis...  5.7 us
  transfers between devices with their start and end apart: 5, of which 4 were waited for; matrix products, arithmetic and copies ran while one was open for 19% of the time, Pallas kernels for 0%

profile of v1, /device:TPU:1, one launch (start us, length us, event | category | flops | bytes accessed | tf_op | source)
XLA Modules:
  0.0 221.3 jit_solution(17670499168763801336)
XLA Ops:
  3.2 11.9 %all-to-all-start = ((bf16[32,4,1024]{2,1,0:T(4,128)(2,1)}), bf16[32,4,1024]{2,1,0:T(4,128)(2,1)S(1)}, u32[]{:S(2)}, u32[]{:S(2)}) async-start(bf16[32,4,1024]{2,1,0:T(4,128)(2,1)} %broadcast_in_dim.20), calls=%async_computation | async-start | bytes 524288 | tf_op jit(solution)/shard_map/all_to_all | solution.py:14
  15.0 3.3 %convert_reduce_fusion = f32[4,92]{0,1:T(8,128)S(1)} fusion(bf16[4,92,4096]{2,0,1:T(4,128)(2,1)} %param.7), kind=kLoop, calls=%fused_computation.1 | loop fusion | flops 3014288 | bytes 3016128 | tf_op jit(solution)/shard_map/reduce_sum | solution.py:89
  20.4 3.2 %fusion.4 = bf16[4,92,4096]{2,0,1:T(4,128)(2,1)S(1)} fusion(bf16[4,92,4096]{2,0,1:T(4,128)(2,1)S(1)} %copy-done.1, f32[4096]{0:T(1024)S(1)} %copy-done.4, f32[4,92]{0,1:T(8,128)S(1)} %add_rsqrt_fusion, f32[4,92]{0,1:T(8,128)S(1)} %broadcast_multiply_fusion), kind=kLoop, calls=%fused_computation.6 | loop fusion | flops 7536640 | bytes 6048640 | tf_op jit(solution)/shard_map/convert_element_type | solution.py:92
  23.7 3.3 %copy.29 = bf16[4,92,4096]{2,1,0:T(8,128)(2,1)} copy(bf16[4,92,4096]{2,0,1:T(4,128)(2,1)S(1)} %fusion.4) | data formatting | bytes 6029312 | tf_op jit(solution)/shard_map/convert_element_type | solution.py:92
  27.0 3.4 %reshape.133 = bf16[368,4096]{1,0:T(8,128)(2,1)} reshape(bf16[4,92,4096]{2,1,0:T(8,128)(2,1)} %copy.29) | data formatting | bytes 6029312 | tf_op jit(solution)/shard_map/reshape | solution.py:93
  30.4 9.0 %fusion.11 = f32[368,1024]{1,0:T(8,128)} fusion(bf16[368,4096]{1,0:T(8,128)(2,1)} %reshape.133, bf16[4096,1024]{1,0:T(8,128)(2,1)} %param.9), kind=kOutput, calls=%fused_computation.14 | convolution fusion | flops 3090022400 | bytes 12910592 | tf_op jit(solution)/shard_map/dot_general | solution.py:95
  39.3 2.7 %reshape.134 = f32[4,92,1024]{2,1,0:T(8,128)} reshape(f32[368,1024]{1,0:T(8,128)} %fusion.11) | data formatting | bytes 3014656 | tf_op jit(solution)/shard_map/reshape | solution.py:97
  44.3 19.8 %all_to_all.48 = bf16[32,4,1024]{2,1,0:T(4,128)(2,1)S(1)} all-to-all(bf16[32,4,1024]{2,1,0:T(4,128)(2,1)S(1)} %broadcast_in_dim.22), channel_id=1, replica_groups=mesh['dp_0'=8,'dp_1'=4,'dp_2'=4,'dp_3'=2] {'dp_0','dp_1'}, dimensions={0} | all-to-all | bytes 524288 | tf_op jit(solution)/shard_map/all_to_all | solution.py:14
  64.8 33.8 %all_to_all.49 = bf16[8,32,4,1024]{3,2,1,0:T(4,128)(2,1)} all-to-all(bf16[8,32,4,1024]{3,2,1,0:T(4,128)(2,1)S(1)} %broadcast_in_dim.21), channel_id=1, replica_groups=mesh['dp_0'=8,'dp_1'=4,'dp_2'=4,'dp_3'=2] {'dp_2','dp_3'}, dimensions={0} | all-to-all | bytes 4194304 | tf_op jit(solution)/shard_map/all_to_all | solution.py:14
  100.6 5.4 %all-to-all-start.3 = ((bf16[8,32,4,1024]{3,2,1,0:T(4,128)(2,1)}), bf16[8,32,4,1024]{3,2,1,0:T(4,128)(2,1)}, u32[]{:S(2)}, u32[]{:S(2)}) async-start(bf16[8,32,4,1024]{3,2,1,0:T(4,128)(2,1)} %broadcast_in_dim.23), calls=%async_computation.3 | async-start | bytes 4194304 | tf_op jit(solution)/shard_map/all_to_all | solution.py:14
  106.7 4.1 %copy.30 = bf16[32,8,4,1024]{3,2,1,0:T(4,128)(2,1)} copy(bf16[32,8,4,1024]{3,2,0,1:T(4,128)(2,1)} %bitcast.33) | data formatting | bytes 4194304 | tf_op jit(solution)/shard_map/transpose | solution.py:28
  110.8 4.0 %reshape_reshape.6 = bf16[1024,1024]{1,0:T(8,128)(2,1)} reshape(bf16[32,8,4,1024]{3,2,1,0:T(4,128)(2,1)} %copy.30) | data formatting | bytes 4194304 | tf_op jit(solution)/shard_map/reshape;reshape | solution.py:22
  114.8 17.6 %all-to-all-done.3 = bf16[8,32,4,1024]{3,2,1,0:T(4,128)(2,1)} async-done(((bf16[8,32,4,1024]{3,2,1,0:T(4,128)(2,1)}), bf16[8,32,4,1024]{3,2,1,0:T(4,128)(2,1)}, u32[]{:S(2)}, u32[]{:S(2)}) %all-to-all-start.3) | async-done | bytes 2097184 | tf_op jit(solution)/shard_map/all_to_all | solution.py:14
  132.4 4.1 %copy.31 = bf16[32,8,4,1024]{3,2,1,0:T(4,128)(2,1)} copy(bf16[32,8,4,1024]{3,2,0,1:T(4,128)(2,1)} %bitcast.2) | data formatting | bytes 4194304 | tf_op jit(solution)/shard_map/transpose | solution.py:28
  136.4 4.0 %reshape_reshape.7 = bf16[1024,1024]{1,0:T(8,128)(2,1)} reshape(bf16[32,8,4,1024]{3,2,1,0:T(4,128)(2,1)} %copy.31) | data formatting | bytes 4194304 | tf_op jit(solution)/shard_map/reshape;reshape | solution.py:22
  140.4 2.5 %fusion.38 = (f32[4]{0:T(128)S(1)}, f32[4,1024]{1,0:T(4,128)S(1)}) fusion(bf16[4,1024]{1,0:T(4,128)(2,1)S(1)} %get-tuple-element.14, bf16[1024,1024]{1,0:T(8,128)(2,1)} %reshape_reshape.6, f32[]{:T(128)} %bitcast.29), kind=kOutput, calls=%fused_computation.74 | convolution fusion | flops 8396796 | bytes 2121748 | tf_op jit(solution)/shard_map/dot_general | solution.py:101
  145.9 3.8 %all-to-all-start.4 = ((f32[32,1,4]{2,1,0:T(1,128)}), f32[32,1,4]{2,1,0:T(1,128)S(1)}, u32[]{:S(2)}, u32[]{:S(2)}) async-start(f32[32,1,4]{2,1,0:T(1,128)} %broadcast_in_dim.25), calls=%async_computation.4 | async-start | bytes 32768 | tf_op jit(solution)/shard_map/all_to_all | solution.py:14
  149.7 8.5 %all-to-all-done.4 = f32[32,1,4]{2,1,0:T(1,128)S(1)} async-done(((f32[32,1,4]{2,1,0:T(1,128)}), f32[32,1,4]{2,1,0:T(1,128)S(1)}, u32[]{:S(2)}, u32[]{:S(2)}) %all-to-all-start.4) | async-done | bytes 544 | tf_op jit(solution)/shard_map/all_to_all | solution.py:14
  159.0 5.5 %all-to-all-start.5 = ((f32[8,1,128]{2,1,0:T(1,128)}), f32[8,1,128]{2,1,0:T(1,128)S(1)}, u32[]{:S(2)}, u32[]{:S(2)}) async-start(f32[8,1,128]{2,1,0:T(1,128)} %reshape.139), calls=%async_computation.5 | async-start | bytes 8192 | tf_op jit(solution)/shard_map/all_to_all | solution.py:14
  166.4 2.6 %all-to-all-done.5 = f32[8,1,128]{2,1,0:T(1,128)S(1)} async-done(((f32[8,1,128]{2,1,0:T(1,128)}), f32[8,1,128]{2,1,0:T(1,128)S(1)}, u32[]{:S(2)}, u32[]{:S(2)}) %all-to-all-start.5) | async-done | bytes 4128 | tf_op jit(solution)/shard_map/all_to_all | solution.py:14
  169.8 5.7 %all-to-all-start.6 = ((f32[256,4,2]{1,2,0:T(2,128)}), f32[256,4,2]{1,2,0:T(2,128)S(1)}, u32[]{:S(2)}, u32[]{:S(2)}) async-start(f32[256,4,2]{1,2,0:T(2,128)} %stack.2), calls=%async_computation.6 | async-start | bytes 524288 | tf_op jit(solution)/shard_map/all_to_all | solution.py:37
  179.9 11.1 %all-to-all-done.6 = f32[256,4,2]{1,2,0:T(2,128)S(1)} async-done(((f32[256,4,2]{1,2,0:T(2,128)}), f32[256,4,2]{1,2,0:T(2,128)S(1)}, u32[]{:S(2)}, u32[]{:S(2)}) %all-to-all-start.6) | async-done | bytes 8224 | tf_op jit(solution)/shard_map/all_to_all | solution.py:37
  195.4 8.0 %all_to_all.50 = f32[8,1,2]{2,1,0:T(1,128)S(1)} all-to-all(f32[8,1,2]{2,1,0:T(1,128)S(1)} %broadcast_in_dim.28), channel_id=1, replica_groups=mesh['dp_0'=8,'dp_1'=4,'dp_2'=4,'dp_3'=2] {'dp_2','dp_3'}, dimensions={0} | all-to-all | bytes 128 | tf_op jit(solution)/shard_map/all_to_all | solution.py:14
  203.5 11.6 %all_to_all.51 = f32[32,1,2]{2,1,0:T(1,128)S(1)} all-to-all(f32[32,1,2]{2,1,0:T(1,128)S(1)} %broadcast_in_dim.29), channel_id=1, replica_groups=mesh['dp_0'=8,'dp_1'=4,'dp_2'=4,'dp_3'=2] {'dp_0','dp_1'}, dimensions={0} | all-to-all | bytes 512 | tf_op jit(solution)/shard_map/all_to_all | solution.py:14
  (60 shorter events, 23.5 us)
Async XLA Ops:
  0.6 42.9 %copy-start = (bf16[1024,1024]{1,0:T(8,128)(2,1)S(1)}, bf16[1024,1024]{1,0:T(8,128)(2,1)}, u32[]{:S(2)}) copy-start(bf16[1024,1024]{1,0:T(8,128)(2,1)} %param.10) | copy-start | bytes 6291460
  3.2 41.0 %all-to-all-start = ((bf16[32,4,1024]{2,1,0:T(4,128)(2,1)}), bf16[32,4,1024]{2,1,0:T(4,128)(2,1)S(1)}, u32[]{:S(2)}, u32[]{:S(2)}) async-start(bf16[32,4,1024]{2,1,0:T(4,128)(2,1)} %broadcast_in_dim.20), calls=%async_computation | async-start | bytes 524288 | tf_op jit(solution)/shard_map/all_to_all | solution.py:14
  15.0 3.3 %copy-start.1 = (bf16[4,92,4096]{2,0,1:T(4,128)(2,1)S(1)}, bf16[4,92,4096]{2,0,1:T(4,128)(2,1)}, u32[]{:S(2)}) copy-start(bf16[4,92,4096]{2,0,1:T(4,128)(2,1)} %param.7) | copy-start | bytes 9043972
  18.3 2.1 copy-start.4
  100.6 6.1 %copy-start.5 = (s32[4]{0:T(128)S(1)}, s32[4]{0:T(128)}, u32[]{:S(2)}) copy-start(s32[4]{0:T(128)} %param.12) | copy-start | bytes 52
  100.6 31.8 %all-to-all-start.3 = ((bf16[8,32,4,1024]{3,2,1,0:T(4,128)(2,1)}), bf16[8,32,4,1024]{3,2,1,0:T(4,128)(2,1)}, u32[]{:S(2)}, u32[]{:S(2)}) async-start(bf16[8,32,4,1024]{3,2,1,0:T(4,128)(2,1)} %broadcast_in_dim.23), calls=%async_computation.3 | async-start | bytes 4194304 | tf_op jit(solution)/shard_map/all_to_all | solution.py:14
  140.4 2.5 %copy-start.2 = (bf16[1024,1024]{1,0:T(8,128)(2,1)S(1)}, bf16[1024,1024]{1,0:T(8,128)(2,1)}, u32[]{:S(2)}) copy-start(bf16[1024,1024]{1,0:T(8,128)(2,1)} %reshape_reshape.7) | copy-start | bytes 6291460
  145.9 12.4 %all-to-all-start.4 = ((f32[32,1,4]{2,1,0:T(1,128)}), f32[32,1,4]{2,1,0:T(1,128)S(1)}, u32[]{:S(2)}, u32[]{:S(2)}) async-start(f32[32,1,4]{2,1,0:T(1,128)} %broadcast_in_dim.25), calls=%async_computation.4 | async-start | bytes 32768 | tf_op jit(solution)/shard_map/all_to_all | solution.py:14
  159.0 32.2 %copy-start.3 = (bf16[4,1024]{1,0:T(4,128)(2,1)S(1)}, bf16[4,1024]{1,0:T(4,128)(2,1)}, u32[]{:S(2)}) copy-start(bf16[4,1024]{1,0:T(4,128)(2,1)} %param.11) | copy-start | bytes 24580
  159.0 10.0 %all-to-all-start.5 = ((f32[8,1,128]{2,1,0:T(1,128)}), f32[8,1,128]{2,1,0:T(1,128)S(1)}, u32[]{:S(2)}, u32[]{:S(2)}) async-start(f32[8,1,128]{2,1,0:T(1,128)} %reshape.139), calls=%async_computation.5 | async-start | bytes 8192 | tf_op jit(solution)/shard_map/all_to_all | solution.py:14
  169.8 21.1 %all-to-all-start.6 = ((f32[256,4,2]{1,2,0:T(2,128)}), f32[256,4,2]{1,2,0:T(2,128)S(1)}, u32[]{:S(2)}, u32[]{:S(2)}) async-start(f32[256,4,2]{1,2,0:T(2,128)} %stack.2), calls=%async_computation.6 | async-start | bytes 524288 | tf_op jit(solution)/shard_map/all_to_all | solution.py:37
